TPU v7x, 32 devices: a whole 2x2x4 slice. The times are simulated.
32 devices in a mesh: grp: 2 (over y), seq: 4 (over z), head: 2 (over x), sub: 2 (over core).
Axes of the slice: x: 2, y: 2, z: 4, core: 2. Of those that a mesh axis runs over, the one named last changes fastest.
Arguments:
- latents: bfloat16 [8, 256, 1152], P(('grp', 'seq'), ('head', 'sub')), parts along dimension 0, may hold values from -6 to 6
- timestep: int32 [2], P('grp'), parts along dimension 0, may hold values from 0 to 29
- time_table: float32 [30, 3, 1152], replicated, may hold values from -3 to 3
- shift_table: float32 [2, 3, 1152], replicated, may hold values from -2 to 2
- qkv_weight: bfloat16 [2, 1152, 16, 216], P(None, None, ('head', 'sub')), may hold values from -0.1875 to 0.1875
- norm_gains: float32 [2, 2, 72], replicated, may hold values from 0.1 to 1.9
- out_weight: bfloat16 [2, 1152, 1152], P(None, ('head', 'sub')), may hold values from -0.1875 to 0.1875
Outputs:
- mixed: bfloat16 [8, 256, 1152], P(('grp', 'seq'), ('head', 'sub')), parts along dimension 0
There are 2 independent parts, one for each index of `grp`. A program takes and returns all parts, laid end to end along the dimension named above; an argument that names none is the same for every part. Nothing has to cross between parts.
All inputs are finite; a program needn't handle non-finite values.
Results may differ from a plain program's by a relative error of at most 0.0095.
Values may be sent and summed in bfloat16 or wider, within the bound.
A program may use at most 64 MiB of HBM per device.

v0:
```python
import jax
import jax.numpy as jnp
from jax import lax
from jax.sharding import PartitionSpec as P

EPSILON = 1e-06


def modulate(values, shift_row, scale_row):
    widened = values.astype(jnp.float32)
    center = jnp.mean(widened, axis=-1, keepdims=True)
    spread = jnp.mean(jnp.square(widened - center), axis=-1, keepdims=True)
    normal = (widened - center) * lax.rsqrt(spread + EPSILON)
    return (normal * (1.0 + scale_row) + shift_row).astype(jnp.bfloat16)


def rms_gain(values, gain_row):
    return (
        values
        * lax.rsqrt(jnp.mean(jnp.square(values), axis=-1, keepdims=True) + EPSILON)
        * gain_row
    )


def project(normed, weight, gain_pair):
    leading = normed.shape[:-1]
    head_count = weight.shape[1]
    head_dim = weight.shape[2] // 3
    flattened = jnp.dot(
        normed.reshape(-1, normed.shape[-1]),
        weight.reshape(weight.shape[0], -1),
        preferred_element_type=jnp.float32,
    )
    pieces = flattened.reshape(leading + (head_count, 3, head_dim))
    queries = rms_gain(pieces[..., 0, :], gain_pair[0])
    key_part = rms_gain(pieces[..., 1, :], gain_pair[1])
    return jnp.concatenate([queries, key_part, pieces[..., 2, :]], axis=-1).astype(jnp.bfloat16)


def attend(packed):
    head_dim = packed.shape[-1] // 3
    queries = packed[..., :head_dim]
    key_part = packed[..., head_dim : 2 * head_dim]
    value_part = packed[..., 2 * head_dim :]
    count = queries.shape[0]
    block = 512 if count % 512 == 0 else count
    blocks = queries.reshape((count // block, block) + queries.shape[1:])

    def one_block(query_block):
        scores = jnp.einsum(
            "qhd,khd->hqk", query_block, key_part, preferred_element_type=jnp.float32
        ) * head_dim ** (-0.5)
        exponent = jnp.exp(scores)
        weights = (exponent / jnp.sum(exponent, axis=-1, keepdims=True)).astype(jnp.bfloat16)
        return jnp.einsum(
            "hqk,khd->qhd", weights, value_part, preferred_element_type=jnp.float32
        ).astype(jnp.bfloat16)

    result = lax.map(one_block, blocks)
    return result.reshape((count,) + result.shape[2:])


def body(latents, timestep, time_table, shift_table, qkv_weight, norm_gains, out_weight):
    feature_width = latents.shape[2]
    chosen = (jnp.arange(time_table.shape[0]) == timestep[0])[:, None, None]
    shared = jnp.sum(jnp.where(chosen, time_table, 0.0), axis=0)
    modulation = shared[None] + shift_table

    def gathered_heads(normed, layer_index):
        return project(
            lax.all_gather(normed, ("head", "sub"), axis=1, tiled=True),
            qkv_weight[layer_index],
            norm_gains[layer_index],
        )

    def back_to_tokens(attended, layer_index):
        merged = attended.reshape(attended.shape[0], attended.shape[1], -1)
        all_heads = lax.all_to_all(merged, ("head", "sub"), split_axis=1, concat_axis=2, tiled=True)
        row_block = all_heads.reshape(-1, all_heads.shape[-1])
        summed = jnp.dot(
            row_block,
            lax.all_gather(out_weight[layer_index], ("head", "sub"), axis=0, tiled=True),
            preferred_element_type=jnp.float32,
        )
        return summed.reshape(all_heads.shape[0], all_heads.shape[1], feature_width)

    normed = modulate(latents, modulation[0, 0], modulation[0, 1])
    packed = gathered_heads(normed, 0)
    attended = lax.map(attend, packed)
    update = back_to_tokens(attended, 0)
    current = (latents.astype(jnp.float32) + modulation[0, 2] * update).astype(jnp.bfloat16)
    shifted_rows = lax.all_to_all(current, "seq", split_axis=1, concat_axis=0, tiled=True)
    packed = gathered_heads(modulate(shifted_rows, modulation[1, 0], modulation[1, 1]), 1)
    attended = jax.vmap(attend, in_axes=1, out_axes=1)(packed)
    update = back_to_tokens(attended, 1)
    result = (shifted_rows.astype(jnp.float32) + modulation[1, 2] * update).astype(jnp.bfloat16)
    return lax.all_to_all(result, "seq", split_axis=0, concat_axis=1, tiled=True)


def solution(mesh):
    return jax.shard_map(
        body,
        mesh=mesh,
        in_specs=(
            P(("grp", "seq"), ("head", "sub"), None),
            P("grp"),
            P(),
            P(),
            P(None, None, ("head", "sub"), None),
            P(),
            P(None, ("head", "sub"), None),
        ),
        out_specs=P(("grp", "seq"), ("head", "sub"), None),
        check_vma=False,
    )
```

profile of v0, /device:TPU:0, one launch (start us, length us, event | category | flops | bytes accessed | tf_op | source)
XLA Modules:
  0.0 99.6 jit_solution(3621725734920662956)
XLA Ops:
  6.5 2.5 %fusion.61 = (bf16[1,288,1152]{2,1,0:T(8,128)(2,1)}, bf16[1,288,1152]{2,1,0:T(8,128)(2,1)}) fusion(bf16[2,288,1152]{2,1,0:T(8,128)(2,1)} %param.13), kind=kLoop, calls=%fused_computation.89 | loop fusion | bytes 2654208 | tf_op jit(solution)/shard_map/slice | solution.py:82
  10.5 9.0 %all_gather.12 = bf16[1,256,1152]{2,1,0:T(8,128)(2,1)S(1)} all-gather(bf16[1,64,1152]{2,1,0:T(8,128)(2,1)S(1)} %fusion.36), channel_id=1, replica_groups=mesh['grp'=2,'seq'=4,'head'=2,'sub'=2] {'head','sub'}, dimensions={1}, use_global_device_ids=true | all-gather | bytes 737280 | tf_op jit(solution)/shard_map/all_gather | solution.py:71
  19.5 4.1 %fusion.60 = (bf16[1,1152,4,216]{1,3,2,0:T(8,128)(2,1)}, bf16[1,1152,4,216]{1,3,2,0:T(8,128)(2,1)S(1)}) fusion(bf16[2,1152,4,216]{1,3,2,0:T(8,128)(2,1)} %param.11), kind=kLoop, calls=%fused_computation.88 | loop fusion | bytes 7962624 | tf_op jit(solution)/shard_map/slice | solution.py:72
  23.6 0.8 convolution_bitcast_fusion
  24.5 0.4 fusion.25
  24.9 0.3 convolution_convert_fusion.1
  25.3 0.4 copy.35
  25.7 0.5 broadcast.178
  26.2 1.9 %reduce.20 = bf16[256,288]{1,0:T(8,128)(2,1)S(1)} reduce(bf16[256,1,288]{2,1,0:T(2,128)(2,1)S(1)} %bitcast.139, bf16[]{:T(256)} %broadcast.178), dimensions={1}, to_apply=%bitcast.118.reduce_sub_computation | reduce | bytes 294914
  28.1 0.3 reshape.234
  28.4 9.1 %all_to_all.51 = bf16[4,2,9216]{2,1,0:T(2,128)(2,1)S(1)} all-to-all(bf16[4,2,9216]{2,1,0:T(2,128)(2,1)S(1)} %reshape.234), channel_id=1, replica_groups=mesh['grp'=2,'seq'=4,'head'=2,'sub'=2] {'head','sub'}, dimensions={0} | all-to-all | bytes 294912 | tf_op jit(solution)/shard_map/all_to_all | solution.py:78
  37.5 0.4 reshape.235
  38.2 1.1 %all-gather.5.cloned.1.call-done = bf16[1,1152,1152]{2,1,0:T(8,128)(2,1)} async-done(((bf16[1,288,1152]{2,1,0:T(8,128)(2,1)}), bf16[1,1152,1152]{2,1,0:T(8,128)(2,1)}) %all-gather.5.cloned.1.call-update) | async-done | bytes 2654224 | tf_op jit(solution)/shard_map/all_gather | solution.py:82
  39.3 2.3 %fusion.19 = bf16[1,64,1152]{2,1,0:T(8,128)(2,1)S(1)} fusion(bf16[64,1152]{1,0:T(8,128)(2,1)S(1)} %reshape.218, bf16[1,1152,1152]{2,1,0:T(8,128)(2,1)} %all-gather.5.cloned.1.call-done, bf16[1,64,1152]{2,1,0:T(8,128)(2,1)S(1)} %copy-done, f32[1152]{0:T(1024)S(1)} %get-tuple-element.58), kind=kOutput, calls=%fused_computation.9 | convolution fusion | flops 170164224 | bytes 3101184 | tf_op jit(solution)/shard_map/dot_general | solution.py:80
  41.9 1.5 %reduce.21 = bf16[64,1152]{1,0:T(8,128)(2,1)S(1)} reduce(bf16[64,1,1152]{2,1,0:T(2,128)(2,1)S(1)} %bitcast.140, bf16[]{:T(256)} %broadcast.178), dimensions={1}, to_apply=%bitcast.131.reduce_sub_computation | reduce | bytes 294914
  43.4 0.7 reshape.236
  44.1 4.6 %all-to-all-start.1 = ((bf16[4,2,9216]{2,1,0:T(2,128)(2,1)}), bf16[4,2,9216]{2,1,0:T(2,128)(2,1)S(1)}, u32[]{:S(2)}, u32[]{:S(2)}) async-start(bf16[4,2,9216]{2,1,0:T(2,128)(2,1)} %reshape.236), calls=%async_computation.1 | async-start | bytes 294912 | tf_op jit(solution)/shard_map/all_to_all | solution.py:92
  48.7 0.7 all-gather.7.cloned.1.call-update
  49.4 5.8 %all-to-all-done.1 = bf16[4,2,9216]{2,1,0:T(2,128)(2,1)S(1)} async-done(((bf16[4,2,9216]{2,1,0:T(2,128)(2,1)}), bf16[4,2,9216]{2,1,0:T(2,128)(2,1)S(1)}, u32[]{:S(2)}, u32[]{:S(2)}) %all-to-all-start.1) | async-done | bytes 147488 | tf_op jit(solution)/shard_map/all_to_all | solution.py:92
  55.3 0.6 convert_reduce_fusion.1
  56.0 1.0 %multiply_reduce_fusion.2 = f32[64]{0:T(128)S(1)} fusion(f32[64]{0:T(128)S(1)} %broadcast_multiply_fusion, bf16[64,1,1152]{2,1,0:T(2,128)(2,1)S(1)} %reshape.237), kind=kLoop, calls=%fused_computation.46 | loop fusion | flops 294848 | bytes 147968 | tf_op jit(solution)/shard_map/reduce_sum | solution.py:12
  57.2 9.7 %all_gather.14 = bf16[4,64,1152]{2,1,0:T(8,128)(2,1)S(1)} all-gather(bf16[4,16,1152]{2,1,0:T(8,128)(2,1)S(1)} %add_convert_fusion), channel_id=1, replica_groups=mesh['grp'=2,'seq'=4,'head'=2,'sub'=2] {'head','sub'}, dimensions={1}, use_global_device_ids=true | all-gather | bytes 737280 | tf_op jit(solution)/shard_map/all_gather | solution.py:71
  66.9 2.8 %fusion.27 = f32[4,64,4,3,72]{4,1,3,2,0:T(8,128)S(1)} fusion(bf16[4,3,72,1152,1]{3,2,1,0,4:T(8,128)(2,1)} %bitcast.137, bf16[4,64,1152]{2,1,0:T(8,128)(2,1)S(1)} %all_gather.14), kind=kOutput, calls=%fused_computation.18 | convolution fusion | flops 509607936 | bytes 3465216 | tf_op jit(solution)/shard_map/dot_general | solution.py:29
  69.7 0.4 multiply_reduce_fusion.1
  70.1 0.3 fusion.41
  70.5 0.5 fusion.45
  70.9 0.3 copy.40
  71.7 0.4 fusion.26
  72.5 7.9 %all_to_all.52 = bf16[4,64,288]{2,0,1:T(4,128)(2,1)S(1)} all-to-all(bf16[4,64,288]{2,0,1:T(4,128)(2,1)S(1)} %reshape.227), channel_id=1, replica_groups=mesh['grp'=2,'seq'=4,'head'=2,'sub'=2] {'head','sub'}, dimensions={1} | all-to-all | bytes 294912 | tf_op jit(solution)/shard_map/all_to_all | solution.py:78
  80.7 2.3 %fusion.22 = bf16[4,16,1152]{2,1,0:T(8,128)(2,1)S(1)} fusion(f32[4,16,1152]{2,1,0:T(8,128)S(1)} %bitcast.136, bf16[4,16,1152]{2,1,0:T(8,128)(2,1)S(1)} %dot_general.54, bf16[1,1152,1152]{2,1,0:T(8,128)(2,1)} %all-gather.7.cloned.1.call-done, f32[1152]{0:T(1024)S(1)} %get-tuple-element.46), kind=kOutput, calls=%fused_computation.10 | convolution fusion | flops 170090496 | bytes 3248640 | tf_op jit(solution)/shard_map/dot_general | solution.py:80
  83.0 9.0 %all_to_all.53 = bf16[4,16,1152]{2,1,0:T(8,128)(2,1)S(1)} all-to-all(bf16[4,16,1152]{2,1,0:T(8,128)(2,1)S(1)} %fusion.22), channel_id=1, replica_groups=mesh['grp'=2,'seq'=4,'head'=2,'sub'=2] {'seq'}, dimensions={0} | all-to-all | bytes 294912 | tf_op jit(solution)/shard_map/all_to_all | solution.py:97
  92.1 0.7 copy.64
  (46 shorter events, 2.9 us)
Async XLA Ops:
  6.5 3.2 %copy-start.1 = (f32[30,3,1152]{2,0,1:T(8,128)S(1)}, f32[30,3,1152]{2,0,1:T(8,128)}, u32[]{:S(2)}) copy-start(f32[30,3,1152]{2,0,1:T(8,128)} %param.9) | copy-start | bytes 1244164
  6.5 3.4 %copy-start.2 = (f32[2,3,1152]{2,0,1:T(2,128)S(1)}, f32[2,3,1152]{2,0,1:T(2,128)}, u32[]{:S(2)}) copy-start(f32[2,3,1152]{2,0,1:T(2,128)} %param.10) | copy-start | bytes 82948
  6.5 3.5 %copy-start = (bf16[1,64,1152]{2,1,0:T(8,128)(2,1)S(1)}, bf16[1,64,1152]{2,1,0:T(8,128)(2,1)}, u32[]{:S(2)}) copy-start(bf16[1,64,1152]{2,1,0:T(8,128)(2,1)} %param.7) | copy-start | bytes 442372
  6.5 32.7 %all-gather.5.cloned.1.call-start = ((), (), s32[]{:S(2)}) async-start(), calls=%async_computation.4 | async-start | bytes 3317760 | tf_op jit(solution)/shard_map/all_gather | solution.py:82
  23.6 0.9 copy-start.3
  44.1 11.1 %all-to-all-start.1 = ((bf16[4,2,9216]{2,1,0:T(2,128)(2,1)}), bf16[4,2,9216]{2,1,0:T(2,128)(2,1)S(1)}, u32[]{:S(2)}, u32[]{:S(2)}) async-start(bf16[4,2,9216]{2,1,0:T(2,128)(2,1)} %reshape.236), calls=%async_computation.1 | async-start | bytes 294912 | tf_op jit(solution)/shard_map/all_to_all | solution.py:92
  48.7 32.0 %all-gather.7.cloned.1.call-start = ((), (), s32[]{:S(2)}) async-start(), calls=%async_computation.5 | async-start | bytes 3317760 | tf_op jit(solution)/shard_map/all_gather | solution.py:82
Sparse Core Ops, SparseCore 0:
  9.2 30.0 all-gather.4
  51.0 27.7 all-gather.6
where the time goes:
time: 100 us; the launch traced here: 99.6 us
  blocking collectives  44.7 us (45%)
  between operations  14.3 us (14%)
  local copies, waits for them, and re-layouts  11.8 us (12%)
  matrix products  9.85 us (10%)
  waiting for transfers between devices  7.63 us (8%)
  other arithmetic  6.69 us (7%)
  starting transfers between devices  4.6 us (5%)
    all_gather x2, blocking collectives, gathered_heads(): lax.all_gather(normed, ('head', 'sub'), axis=1, tiled=True)  18.7 us
    all_to_all x2, blocking collectives, back_to_tokens(): lax.all_to_all(merged, ('head', 'sub'), split_axis=1, concat_axis=2, tile...  16.9 us
    all_to_all x1, blocking collectives, body(): lax.all_to_all(result, 'seq', split_axis=0, concat_axis=1, tiled=True)  9.04 us
    all_to_all x1, waiting for transfers between devices, body(): lax.all_to_all(current, 'seq', split_axis=1, concat_axis=0, tiled=True)  5.79 us
    dot_general x2, matrix products, back_to_tokens(): jnp.dot(row_block, lax.all_gather(out_weight[layer_index], ('head', 'sub'...  4.66 us
    all_to_all x1, starting transfers between devices, body(): lax.all_to_all(current, 'seq', split_axis=1, concat_axis=0, tiled=True)  4.6 us
    slice x1, local copies, waits for them, and re-layouts, gathered_heads(): qkv_weight[layer_index]  4.09 us
    dot_general x2, matrix products, project(): jnp.dot(normed.reshape(-1, normed.shape[-1]), weight.reshape(weight.shape...  3.56 us
  transfers between devices with their start and end apart: 3, of which 2 were waited for; matrix products, arithmetic and copies ran while one was open for 18% of the time, Pallas kernels for 0%

commit v1 on v0

--- a/solution.py
+++ b/solution.py
@@ -1,6 +1,10 @@
+import functools
+
 import jax
 import jax.numpy as jnp
 from jax import lax
+from jax.experimental import pallas as pl
+from jax.experimental.pallas import tpu as pltpu
 from jax.sharding import PartitionSpec as P
 
 EPSILON = 1e-06
@@ -97,9 +101,370 @@
     return lax.all_to_all(result, "seq", split_axis=0, concat_axis=1, tiled=True)
 
 
+MESH = pl.DeviceIdType.MESH
+
+
+def contract(left, right, left_dim, right_dim):
+    return lax.dot_general(
+        left,
+        right,
+        (((left_dim,), (right_dim,)), ((), ())),
+        preferred_element_type=jnp.float32,
+    )
+
+
+def normalize(rows, shift_row, scale_row):
+    center = jnp.mean(rows, axis=-1, keepdims=True)
+    moved = rows - center
+    spread = jnp.mean(jnp.square(moved), axis=-1, keepdims=True)
+    return (moved * lax.rsqrt(spread + EPSILON) * (1.0 + scale_row) + shift_row).astype(jnp.bfloat16)
+
+
+def fused_kernel(
+    seq_size,
+    step_ref,
+    lat_hbm,
+    time_hbm,
+    shift_hbm,
+    qkv_hbm,
+    gain_hbm,
+    proj_hbm,
+    out_ref,
+    lat,
+    time_rows,
+    shift_rows,
+    gain,
+    wq,
+    wo,
+    g0,
+    qkv,
+    att,
+    part0,
+    part1,
+    pair_out,
+    pair_in,
+    cross_out,
+    cross_in,
+    current,
+    seq_out,
+    g1,
+    back_out,
+    back_in,
+    load_sem,
+    send_sem,
+    recv_sem,
+):
+    grp, seq = lax.axis_index("grp"), lax.axis_index("seq")
+    head, sub = lax.axis_index("head"), lax.axis_index("sub")
+    sibling = (grp, seq, head, 1 - sub)
+    across = (grp, seq, 1 - head, sub)
+
+    def along(r):
+        return (grp, lax.rem(seq + r, seq_size), head, sub)
+
+    heads, _, width = wq.shape[1:]
+    head_dim = wq.shape[2] // 3
+    pixels = lat.shape[1]
+    tile = pixels // seq_size
+    tokens = 4 * pixels
+
+    far_first = sorted(range(1, seq_size), key=lambda r: -min(r, seq_size - r))
+    order = far_first + [0]
+    place = {r: i for i, r in enumerate([0] + far_first)}
+
+    loads = []
+    for i, (source, target) in enumerate(
+        [
+            (lat_hbm, lat),
+            (time_hbm, time_rows),
+            (shift_hbm, shift_rows),
+            (gain_hbm, gain),
+            (qkv_hbm.at[0], wq.at[0]),
+            (proj_hbm.at[0], wo.at[0]),
+            (qkv_hbm.at[1], wq.at[1]),
+            (proj_hbm.at[1], wo.at[1]),
+        ]
+    ):
+        load = pltpu.make_async_copy(source, target, load_sem.at[i])
+        load.start()
+        loads.append(load)
+
+    barrier = pltpu.get_barrier_semaphore()
+    peers = [sibling, across] + [along(r) for r in range(1, seq_size)]
+    for peer in peers:
+        pl.semaphore_signal(barrier, inc=1, device_id=peer, device_id_type=MESH)
+
+    started = []
+
+    def send(source, target, device):
+        i = len(started)
+        copy = pltpu.make_async_remote_copy(
+            src_ref=source,
+            dst_ref=target,
+            send_sem=send_sem.at[i],
+            recv_sem=recv_sem.at[i],
+            device_id=device,
+            device_id_type=MESH,
+        )
+        copy.start()
+        started.append(copy)
+        return copy
+
+    for load in loads[:4]:
+        load.wait()
+    step = step_ref[0]
+
+    def modulation(block, j):
+        return time_rows[j, pl.ds(step, 1), :] + shift_rows[j, pl.ds(block, 1), :]
+
+    def chunk_rows(r):
+        start = lax.rem(seq + r, seq_size) * tile
+        return pl.ds(pl.multiple_of(start, tile), tile)
+
+    shift0, scale0, gate0 = (modulation(0, j) for j in range(3))
+    for r in range(seq_size):
+        rows = lat[0, chunk_rows(r), :].astype(jnp.float32)
+        g0[0, pl.ds(r * tile, tile), :] = normalize(rows, shift0, scale0)
+
+    diagonal = lax.broadcasted_iota(jnp.int32, (head_dim, head_dim), 0) == lax.broadcasted_iota(
+        jnp.int32, (head_dim, head_dim), 1
+    )
+
+    def gain_column(block, which):
+        row = gain[block, pl.ds(which, 1), :]
+        return jnp.sum(jnp.where(diagonal, row, 0.0), axis=1, keepdims=True)
+
+    pl.semaphore_wait(barrier, len(peers))
+
+    half = pixels // 2
+    halves = [pl.ds(0, half), pl.ds(half, half)]
+    cross = [send(g0.at[0, part], g0.at[2, part], across) for part in halves]
+    pair = send(g0.at[0], g0.at[1], sibling)
+
+    def project_block(block, values, side):
+        lanes = pl.ds(side * (tokens // 2), tokens // 2)
+        for h in range(heads):
+            flat = contract(wq[block, h], values, 1, 1)
+            for j in range(3):
+                piece = flat[j * head_dim : (j + 1) * head_dim]
+                if j < 2:
+                    mean = jnp.mean(jnp.square(piece), axis=0, keepdims=True)
+                    piece = piece * lax.rsqrt(mean + EPSILON) * gains[block][j]
+                qkv[h, pl.ds(j * head_dim, head_dim), lanes] = piece
+
+    gains = [[gain_column(block, j) for j in range(2)] for block in range(2)]
+    loads[4].wait()
+    pair.wait_recv()
+    project_block(0, g0[0:2].reshape(2 * pixels, width), 0)
+    forwarded = []
+    for part, copy in zip(halves, cross):
+        copy.wait_recv()
+        forwarded.append(send(g0.at[2, part], g0.at[3, part], sibling))
+    for copy in forwarded:
+        copy.wait_recv()
+    project_block(0, g0[2:4].reshape(2 * pixels, width), 1)
+
+    scale = head_dim ** (-0.5)
+    for h in range(heads):
+        queries = qkv[h, 0:head_dim].astype(jnp.bfloat16)
+        keys = qkv[h, head_dim : 2 * head_dim].astype(jnp.bfloat16)
+        values = qkv[h, 2 * head_dim : 3 * head_dim].astype(jnp.bfloat16)
+        exponent = jnp.exp(contract(keys, queries, 0, 0) * scale)
+        total = jnp.sum(exponent, axis=0, keepdims=True)
+        mixed = contract(values, exponent.astype(jnp.bfloat16), 1, 0)
+        att[pl.ds(h * head_dim, head_dim)] = mixed / total
+
+    def reduce_pair(block, part):
+        pairs, crosses = {}, {}
+        for r in order:
+            pair_out[block, r, 0] = part(1, r).astype(jnp.bfloat16)
+            pair_out[block, r, 1] = part(3, r).astype(jnp.bfloat16)
+            pairs[r] = send(pair_out.at[block, r], pair_in.at[block, r], sibling)
+        for r in order:
+            pairs[r].wait_recv()
+            cross_out[block, r] = (part(2, r) + pair_in[block, r, 1].astype(jnp.float32)).astype(jnp.bfloat16)
+            crosses[r] = send(cross_out.at[block, r], cross_in.at[block, r], across)
+        return crosses
+
+    def reduced(block, part, crosses, r):
+        crosses[r].wait_recv()
+        return (
+            part(0, r)
+            + pair_in[block, r, 0].astype(jnp.float32)
+            + cross_in[block, r].astype(jnp.float32)
+        )
+
+    loads[5].wait()
+    part0[...] = contract(att[...].astype(jnp.bfloat16), wo[0], 0, 0).reshape(part0.shape)
+
+    def first_part(slot, r):
+        return part0[slot, r]
+
+    crosses = reduce_pair(0, first_part)
+    shift1, scale1, gate1 = (modulation(1, j) for j in range(3))
+    moves = {}
+    for r in order:
+        update = reduced(0, first_part, crosses, r)
+        rows = (lat[0, chunk_rows(r), :].astype(jnp.float32) + gate0 * update).astype(jnp.bfloat16)
+        current[r] = rows
+        normed = normalize(rows.astype(jnp.float32), shift1, scale1)
+        if r:
+            seq_out[r] = normed
+            moves[r] = send(seq_out.at[r], g1.at[place[r], 0], along(r))
+        else:
+            g1[0, 0] = normed
+
+    loads[6].wait()
+    by_place = [0] + far_first
+    gathered = []
+
+    def spread(i):
+        gathered.append(
+            (
+                send(g1.at[i, 0], g1.at[i, 2], across),
+                send(g1.at[i, 0], g1.at[i, 1], sibling),
+            )
+        )
+
+    relayed = []
+
+    def relay(i):
+        gathered[i][0].wait_recv()
+        relayed.append(send(g1.at[i, 2], g1.at[i, 3], sibling))
+
+    middle = seq_size // 2
+    spread(0)
+    for i in range(1, seq_size):
+        moves[by_place[i]].wait_recv()
+        spread(i)
+        relay(i - 1)
+
+    def ready(places):
+        for i in places:
+            gathered[i][1].wait_recv()
+            relayed[i].wait_recv()
+
+    ready(range(middle))
+    project_block(1, g1[0:middle].reshape(2 * pixels, width), 0)
+    relay(seq_size - 1)
+    ready(range(middle, seq_size))
+    project_block(1, g1[middle:seq_size].reshape(2 * pixels, width), 1)
+
+    for h in range(heads):
+        queries, keys, values = (
+            qkv[h, pl.ds(j * head_dim, head_dim)].astype(jnp.bfloat16).astype(jnp.float32)
+            for j in range(3)
+        )
+        total = jnp.zeros((1, tokens), jnp.float32)
+        mixed = jnp.zeros((head_dim, tokens), jnp.float32)
+        for r in range(seq_size):
+            turn = r * 4 * tile
+            turned_keys = pltpu.roll(keys, turn, 1) if r else keys
+            turned_values = pltpu.roll(values, turn, 1) if r else values
+            exponent = jnp.exp(jnp.sum(queries * turned_keys, axis=0, keepdims=True) * scale)
+            total = total + exponent
+            mixed = mixed + exponent * turned_values
+        att[pl.ds(h * head_dim, head_dim)] = mixed / total
+
+    loads[7].wait()
+    part1[...] = contract(att[...].astype(jnp.bfloat16), wo[1], 0, 0).reshape(part1.shape)
+
+    def second_part(slot, r):
+        return part1[place[r], slot]
+
+    crosses = reduce_pair(1, second_part)
+    returns = {}
+    for r in order:
+        update = reduced(1, second_part, crosses, r)
+        if r:
+            back_out[r] = update.astype(jnp.bfloat16)
+            returns[r] = send(back_out.at[r], back_in.at[r], along(seq_size - r))
+        else:
+            rows = current[r].astype(jnp.float32) + gate1 * update
+            out_ref[0, chunk_rows(r), :] = rows.astype(jnp.bfloat16)
+    for r in far_first:
+        returns[r].wait_recv()
+        rows = current[r].astype(jnp.float32) + gate1 * back_in[r].astype(jnp.float32)
+        out_ref[0, chunk_rows(r), :] = rows.astype(jnp.bfloat16)
+    for copy in started:
+        copy.wait_send()
+
+
+def fused_body(seq_size, latents, timestep, time_table, shift_table, qkv_weight, norm_gains, out_weight):
+    _, pixels, width = latents.shape
+    blocks, _, heads, packed = qkv_weight.shape
+    head_dim = packed // 3
+    tile = pixels // seq_size
+    tokens = 4 * pixels
+    copies = 5 + 2 * 2 * seq_size + 2 * (seq_size - 1) + 3 * seq_size
+    anywhere = pl.BlockSpec(memory_space=pl.ANY)
+    half, full = jnp.bfloat16, jnp.float32
+    vmem = pltpu.VMEM
+    return pl.pallas_call(
+        functools.partial(fused_kernel, seq_size),
+        out_shape=jax.ShapeDtypeStruct(latents.shape, half),
+        in_specs=[pl.BlockSpec(memory_space=pltpu.SMEM)] + [anywhere] * 6,
+        out_specs=pl.BlockSpec(memory_space=pltpu.VMEM),
+        scratch_shapes=[
+            vmem(latents.shape, half),
+            vmem((3, time_table.shape[0], width), full),
+            vmem((3, blocks, width), full),
+            vmem(norm_gains.shape, full),
+            vmem((blocks, heads, packed, width), half),
+            vmem(out_weight.shape, half),
+            vmem((4, pixels, width), half),
+            vmem((heads, packed, tokens), full),
+            vmem((heads * head_dim, tokens), full),
+            vmem((4, seq_size, tile, width), full),
+            vmem((seq_size, 4, tile, width), full),
+            vmem((blocks, seq_size, 2, tile, width), half),
+            vmem((blocks, seq_size, 2, tile, width), half),
+            vmem((blocks, seq_size, tile, width), half),
+            vmem((blocks, seq_size, tile, width), half),
+            vmem((seq_size, tile, width), half),
+            vmem((seq_size, tile, width), half),
+            vmem((seq_size, 4, tile, width), half),
+            vmem((seq_size, tile, width), half),
+            vmem((seq_size, tile, width), half),
+            pltpu.SemaphoreType.DMA((8,)),
+            pltpu.SemaphoreType.DMA((copies,)),
+            pltpu.SemaphoreType.DMA((copies,)),
+        ],
+        compiler_params=pltpu.CompilerParams(
+            collective_id=0, has_side_effects=True, vmem_limit_bytes=48 * 1024 * 1024
+        ),
+    )(
+        timestep,
+        latents,
+        jnp.transpose(time_table, (1, 0, 2)),
+        jnp.transpose(shift_table, (1, 0, 2)),
+        jnp.transpose(qkv_weight, (0, 2, 3, 1)),
+        norm_gains,
+        out_weight,
+    )
+
+
+def chosen_body(mesh, *arrays):
+    sizes = mesh.shape
+    frames, pixels, _ = arrays[0].shape
+    head_dim = arrays[4].shape[3] // 3
+    fits = (
+        sizes["head"] == 2
+        and sizes["sub"] == 2
+        and frames == 1
+        and sizes["seq"] % 2 == 0
+        and pixels % (16 * sizes["seq"]) == 0
+        and pixels % 64 == 0
+        and head_dim % 8 == 0
+    )
+    if fits:
+        return fused_body(sizes["seq"], *arrays)
+    return body(*arrays)
+
+
 def solution(mesh):
     return jax.shard_map(
-        body,
+        functools.partial(chosen_body, mesh),
         mesh=mesh,
         in_specs=(
             P(("grp", "seq"), ("head", "sub"), None),

time: 100 us -> 48.4 us (0.48)
  blocking collectives: 44.7 us -> 0 us
  Pallas kernels: 0 us -> 39.9 us
  between operations: 14.3 us -> 0.67 us
  matrix products: 9.85 us -> 0 us
  waiting for transfers between devices: 7.63 us -> 0 us
  other arithmetic: 6.69 us -> 0 us
  starting transfers between devices: 4.6 us -> 0 us
  local copies, waits for them, and re-layouts: 11.8 us -> 7.45 us
    pallas_call x0 -> x1, Pallas kernels: none -> 39.9 us  [fused_body(): pl.pallas_call(functools.partial(fused_kernel, seq_size), out_shape=jax.S...]
    all_to_all x3 -> x0, blocking collectives: 26 us -> none  [the longest x2 16.9 us: back_to_tokens(): lax.all_to_all(merged, ('head', 'sub'), split_axis=1, concat_axis=2, tile...]
    all_gather x2 -> x0, blocking collectives: 18.7 us -> none  [gathered_heads(): lax.all_gather(normed, ('head', 'sub'), axis=1, tiled=True)]
    dot_general x8 -> x0, matrix products: 9.85 us -> none  [the longest x2 4.66 us: back_to_tokens(): jnp.dot(row_block, lax.all_gather(out_weight[layer_index], ('head', 'sub'...]
    slice x2 -> x0, local copies, waits for them, and re-layouts: 6.64 us -> none  [the longest x1 4.09 us: gathered_heads(): qkv_weight[layer_index]]
    all_to_all x1 -> x0, waiting for transfers between devices: 5.79 us -> none  [body(): lax.all_to_all(current, 'seq', split_axis=1, concat_axis=0, tiled=True)]
    unnamed x16 -> x13, local copies, waits for them, and re-layouts: 2.72 us -> 7.45 us
    all_to_all x1 -> x0, starting transfers between devices: 4.6 us -> none  [body(): lax.all_to_all(current, 'seq', split_axis=1, concat_axis=0, tiled=True)]
  transfers between devices with their start and end apart: 3 -> 0, of which waited for: 2 -> 0; matrix products, arithmetic and copies ran while one was open for 18% -> 0% of each run, Pallas kernels for 0% -> 0%
where the time goes in v1:
time: 48.4 us; the launch traced here: 48 us
  Pallas kernels  39.9 us (82%)
  local copies, waits for them, and re-layouts  7.45 us (15%)
  between operations  0.67 us (1%)
    pallas_call x1, Pallas kernels, fused_body(): pl.pallas_call(functools.partial(fused_kernel, seq_size), out_shape=jax.S...  39.9 us
    unnamed x13, local copies, waits for them, and re-layouts  7.45 us

profile of v1, /device:TPU:0, one launch (start us, length us, event | category | flops | bytes accessed | tf_op | source)
XLA Modules:
  0.0 48.0 jit_solution(5559799701154752653)
XLA Ops:
  0.7 0.0 copy-start
  0.7 2.1 %copy-done = bf16[2,1152,4,216]{1,3,2,0:T(8,128)(2,1)S(1)} copy-done((bf16[2,1152,4,216]{1,3,2,0:T(8,128)(2,1)S(1)}, bf16[2,1152,4,216]{1,3,2,0:T(8,128)(2,1)}, u32[]{:S(2)}) %copy-start) | copy-done | bytes 3981336
  2.8 0.0 copy-start.1
  2.8 1.3 %copy-done.1 = bf16[2,288,1152]{2,1,0:T(8,128)(2,1)S(1)} copy-done((bf16[2,288,1152]{2,1,0:T(8,128)(2,1)S(1)}, bf16[2,288,1152]{2,1,0:T(8,128)(2,1)}, u32[]{:S(2)}) %copy-start.1) | copy-done | bytes 1327128
  4.1 0.0 copy-start.2
  4.1 1.0 %copy-done.2 = f32[30,3,1152]{2,0,1:T(8,128)S(1)} copy-done((f32[30,3,1152]{2,0,1:T(8,128)S(1)}, f32[30,3,1152]{2,0,1:T(8,128)}, u32[]{:S(2)}) %copy-start.2) | copy-done | bytes 414744
  5.1 0.0 copy-start.3
  5.1 0.9 %copy-done.3 = bf16[1,64,1152]{2,1,0:T(8,128)(2,1)S(1)} copy-done((bf16[1,64,1152]{2,1,0:T(8,128)(2,1)S(1)}, bf16[1,64,1152]{2,1,0:T(8,128)(2,1)}, u32[]{:S(2)}) %copy-start.3) | copy-done | bytes 147480
  6.0 0.0 copy-start.4
  6.0 0.7 %copy-done.4 = f32[2,3,1152]{2,0,1:T(2,128)S(1)} copy-done((f32[2,3,1152]{2,0,1:T(2,128)S(1)}, f32[2,3,1152]{2,0,1:T(2,128)}, u32[]{:S(2)}) %copy-start.4) | copy-done | bytes 27672
  6.8 0.0 copy-start.5
  6.8 0.7 %copy-done.5 = f32[2,2,72]{2,1,0:T(2,128)S(1)} copy-done((f32[2,2,72]{2,1,0:T(2,128)S(1)}, f32[2,2,72]{2,1,0:T(2,128)}, u32[]{:S(2)}) %copy-start.5) | copy-done | bytes 1176
  7.5 39.9 %shard_map.73 = bf16[1,64,1152]{2,1,0:T(8,128)(2,1)S(1)} custom-call(s32[1]{0:T(128)S(6)} %copy.9.step_ref, bf16[1,64,1152]{2,1,0:T(8,128)(2,1)S(1)} %copy-done.3, f32[3,30,1152]{2,1,0:T(8,128)S(1)} %bitcast.4, f32[3,2,1152]{2,1,0:T(2,128)S(1)} %bitcast.5, bf16[2,4,216,1152]{3,2,1,0:T(8,128)(2,1)S(1)} %bitcast.3, f32[2,2,72]{2,1,0:T(2,128)S(1)} %copy-done.5, ...), custom_call_target="tpu_custom_call" | custom-call | tf_op jit(solution)/shard_map/pallas_call | solution.py:403
  47.4 0.7 %copy.10 = bf16[1,64,1152]{2,1,0:T(8,128)(2,1)} copy(bf16[1,64,1152]{2,1,0:T(8,128)(2,1)S(1)} %shard_map.73) | data formatting | bytes 294912
Async XLA Ops:
  0.7 2.1 %copy-start = (bf16[2,1152,4,216]{1,3,2,0:T(8,128)(2,1)S(1)}, bf16[2,1152,4,216]{1,3,2,0:T(8,128)(2,1)}, u32[]{:S(2)}) copy-start(bf16[2,1152,4,216]{1,3,2,0:T(8,128)(2,1)} %param.11) | copy-start | bytes 11943940
  2.8 1.3 %copy-start.1 = (bf16[2,288,1152]{2,1,0:T(8,128)(2,1)S(1)}, bf16[2,288,1152]{2,1,0:T(8,128)(2,1)}, u32[]{:S(2)}) copy-start(bf16[2,288,1152]{2,1,0:T(8,128)(2,1)} %proj_hbm.1) | copy-start | bytes 3981316
  4.1 1.0 %copy-start.2 = (f32[30,3,1152]{2,0,1:T(8,128)S(1)}, f32[30,3,1152]{2,0,1:T(8,128)}, u32[]{:S(2)}) copy-start(f32[30,3,1152]{2,0,1:T(8,128)} %param.9) | copy-start | bytes 1244164
  5.1 0.9 %copy-start.3 = (bf16[1,64,1152]{2,1,0:T(8,128)(2,1)S(1)}, bf16[1,64,1152]{2,1,0:T(8,128)(2,1)}, u32[]{:S(2)}) copy-start(bf16[1,64,1152]{2,1,0:T(8,128)(2,1)} %lat_hbm.1) | copy-start | bytes 442372
  6.0 0.7 %copy-start.4 = (f32[2,3,1152]{2,0,1:T(2,128)S(1)}, f32[2,3,1152]{2,0,1:T(2,128)}, u32[]{:S(2)}) copy-start(f32[2,3,1152]{2,0,1:T(2,128)} %param.10) | copy-start | bytes 82948
  6.8 0.7 %copy-start.5 = (f32[2,2,72]{2,1,0:T(2,128)S(1)}, f32[2,2,72]{2,1,0:T(2,128)}, u32[]{:S(2)}) copy-start(f32[2,2,72]{2,1,0:T(2,128)} %gain_hbm.1) | copy-start | bytes 3460

commit v2 on v1

--- a/solution.py
+++ b/solution.py
@@ -431,7 +431,7 @@
             pltpu.SemaphoreType.DMA((copies,)),
         ],
         compiler_params=pltpu.CompilerParams(
-            collective_id=0, has_side_effects=True, vmem_limit_bytes=48 * 1024 * 1024
+            collective_id=0, has_side_effects=True, vmem_limit_bytes=67_043_328
         ),
     )(
         timestep,

time: 48.4 us -> 41.5 us (0.86)
  local copies, waits for them, and re-layouts: 7.45 us -> 1.58 us
  Pallas kernels: 39.9 us -> 39.1 us
    unnamed x13 -> x1, local copies, waits for them, and re-layouts: 7.45 us -> 1.58 us
    pallas_call x1, Pallas kernels: 39.9 us -> 39.1 us  [fused_body(): pl.pallas_call(functools.partial(fused_kernel, seq_size), out_shape=jax.S...]
where the time goes in v2:
time: 41.5 us; the launch traced here: 41.3 us
  Pallas kernels  39.1 us (94%)
  local copies, waits for them, and re-layouts  1.58 us (4%)
  between operations  0.66 us (2%)
    pallas_call x1, Pallas kernels, fused_body(): pl.pallas_call(functools.partial(fused_kernel, seq_size), out_shape=jax.S...  39.1 us
    unnamed x1, local copies, waits for them, and re-layouts  1.58 us

profile of v2, /device:TPU:0, one launch (start us, length us, event | category | flops | bytes accessed | tf_op | source)
XLA Modules:
  0.0 41.3 jit_solution(5030649782909122133)
XLA Ops:
  0.7 39.1 %shard_map.73 = bf16[1,64,1152]{2,1,0:T(8,128)(2,1)} custom-call(s32[1]{0:T(128)S(6)} %copy.9.step_ref, bf16[1,64,1152]{2,1,0:T(8,128)(2,1)} %lat_hbm.1, f32[3,30,1152]{2,1,0:T(8,128)} %bitcast.4, f32[3,2,1152]{2,1,0:T(2,128)} %bitcast.5, bf16[2,4,216,1152]{3,2,1,0:T(8,128)(2,1)} %bitcast.3, f32[2,2,72]{2,1,0:T(2,128)} %gain_hbm.1, ...), custom_call_target="tpu_custom_call" | custom-call | tf_op jit(solution)/shard_map/pallas_call | solution.py:403
  39.7 1.6 %copy.10 = bf16[1,64,1152]{2,1,0:T(8,128)(2,1)} copy(bf16[1,64,1152]{2,1,0:T(8,128)(2,1)} %shard_map.73) | data formatting | bytes 294912

commit v3 on v2

--- a/solution.py
+++ b/solution.py
@@ -122,7 +122,7 @@
 
 def fused_kernel(
     seq_size,
-    step_ref,
+    step_hbm,
     lat_hbm,
     time_hbm,
     shift_hbm,
@@ -130,6 +130,7 @@
     gain_hbm,
     proj_hbm,
     out_ref,
+    step_ref,
     lat,
     time_rows,
     shift_rows,
@@ -141,8 +142,10 @@
     att,
     part0,
     part1,
-    pair_out,
-    pair_in,
+    pair0_out,
+    pair0_in,
+    pair1_out,
+    pair1_in,
     cross_out,
     cross_in,
     current,
@@ -159,8 +162,17 @@
     sibling = (grp, seq, head, 1 - sub)
     across = (grp, seq, 1 - head, sub)
 
+    def partner(r):
+        position = seq
+        bit = 1
+        while bit < seq_size:
+            if r & bit:
+                position = position + bit - 2 * bit * lax.rem(lax.div(seq, bit), 2)
+            bit *= 2
+        return position
+
     def along(r):
-        return (grp, lax.rem(seq + r, seq_size), head, sub)
+        return (grp, partner(r), head, sub)
 
     heads, _, width = wq.shape[1:]
     head_dim = wq.shape[2] // 3
@@ -168,7 +180,7 @@
     tile = pixels // seq_size
     tokens = 4 * pixels
 
-    far_first = sorted(range(1, seq_size), key=lambda r: -min(r, seq_size - r))
+    far_first = list(range(seq_size - 1, 0, -1))
     order = far_first + [0]
     place = {r: i for i, r in enumerate([0] + far_first)}
 
@@ -183,6 +195,7 @@
             (proj_hbm.at[0], wo.at[0]),
             (qkv_hbm.at[1], wq.at[1]),
             (proj_hbm.at[1], wo.at[1]),
+            (step_hbm, step_ref),
         ]
     ):
         load = pltpu.make_async_copy(source, target, load_sem.at[i])
@@ -210,7 +223,7 @@
         started.append(copy)
         return copy
 
-    for load in loads[:4]:
+    for load in loads[:4] + loads[8:]:
         load.wait()
     step = step_ref[0]
 
@@ -218,7 +231,7 @@
         return time_rows[j, pl.ds(step, 1), :] + shift_rows[j, pl.ds(block, 1), :]
 
     def chunk_rows(r):
-        start = lax.rem(seq + r, seq_size) * tile
+        start = partner(r) * tile
         return pl.ds(pl.multiple_of(start, tile), tile)
 
     shift0, scale0, gate0 = (modulation(0, j) for j in range(3))
@@ -265,6 +278,7 @@
     project_block(0, g0[2:4].reshape(2 * pixels, width), 1)
 
     scale = head_dim ** (-0.5)
+
     for h in range(heads):
         queries = qkv[h, 0:head_dim].astype(jnp.bfloat16)
         keys = qkv[h, head_dim : 2 * head_dim].astype(jnp.bfloat16)
@@ -274,37 +288,39 @@
         mixed = contract(values, exponent.astype(jnp.bfloat16), 1, 0)
         att[pl.ds(h * head_dim, head_dim)] = mixed / total
 
-    def reduce_pair(block, part):
-        pairs, crosses = {}, {}
-        for r in order:
-            pair_out[block, r, 0] = part(1, r).astype(jnp.bfloat16)
-            pair_out[block, r, 1] = part(3, r).astype(jnp.bfloat16)
-            pairs[r] = send(pair_out.at[block, r], pair_in.at[block, r], sibling)
-        for r in order:
-            pairs[r].wait_recv()
-            cross_out[block, r] = (part(2, r) + pair_in[block, r, 1].astype(jnp.float32)).astype(jnp.bfloat16)
-            crosses[r] = send(cross_out.at[block, r], cross_in.at[block, r], across)
-        return crosses
-
-    def reduced(block, part, crosses, r):
-        crosses[r].wait_recv()
-        return (
-            part(0, r)
-            + pair_in[block, r, 0].astype(jnp.float32)
-            + cross_in[block, r].astype(jnp.float32)
+    def project_out(block, side, part):
+        lanes = pl.ds(side * (tokens // 2), tokens // 2)
+        partial = contract(att[:, lanes].astype(jnp.bfloat16), wo[block], 0, 0)
+        first = side * (part.shape[0] // 2)
+        part[pl.ds(first, part.shape[0] // 2)] = partial.reshape(
+            (part.shape[0] // 2,) + part.shape[1:]
         )
 
     loads[5].wait()
-    part0[...] = contract(att[...].astype(jnp.bfloat16), wo[0], 0, 0).reshape(part0.shape)
-
-    def first_part(slot, r):
-        return part0[slot, r]
-
-    crosses = reduce_pair(0, first_part)
+    project_out(0, 1, part0)
+    far_pairs = {}
+    for r in order:
+        pair0_out[1, r] = part0[3, r].astype(jnp.bfloat16)
+        far_pairs[r] = send(pair0_out.at[1, r], pair0_in.at[1, r], sibling)
+    project_out(0, 0, part0)
+    pair0_out[0] = part0[1].astype(jnp.bfloat16)
+    near_pair = send(pair0_out.at[0], pair0_in.at[0], sibling)
+    crosses = {}
+    for r in order:
+        far_pairs[r].wait_recv()
+        summed = part0[2, r] + pair0_in[1, r].astype(jnp.float32)
+        cross_out[0, r] = summed.astype(jnp.bfloat16)
+        crosses[r] = send(cross_out.at[0, r], cross_in.at[0, r], across)
+    near_pair.wait_recv()
     shift1, scale1, gate1 = (modulation(1, j) for j in range(3))
     moves = {}
     for r in order:
-        update = reduced(0, first_part, crosses, r)
+        crosses[r].wait_recv()
+        update = (
+            part0[0, r]
+            + pair0_in[0, r].astype(jnp.float32)
+            + cross_in[0, r].astype(jnp.float32)
+        )
         rows = (lat[0, chunk_rows(r), :].astype(jnp.float32) + gate0 * update).astype(jnp.bfloat16)
         current[r] = rows
         normed = normalize(rows.astype(jnp.float32), shift1, scale1)
@@ -337,7 +353,8 @@
     for i in range(1, seq_size):
         moves[by_place[i]].wait_recv()
         spread(i)
-        relay(i - 1)
+    for i in range(seq_size - 1):
+        relay(i)
 
     def ready(places):
         for i in places:
@@ -367,18 +384,30 @@
         att[pl.ds(h * head_dim, head_dim)] = mixed / total
 
     loads[7].wait()
-    part1[...] = contract(att[...].astype(jnp.bfloat16), wo[1], 0, 0).reshape(part1.shape)
-
-    def second_part(slot, r):
-        return part1[place[r], slot]
-
-    crosses = reduce_pair(1, second_part)
+    pairs, crosses = {}, {}
+    for side in range(2):
+        project_out(1, side, part1)
+        for i in range(side * middle, (side + 1) * middle):
+            r = by_place[i]
+            pair1_out[r, 0] = part1[i, 1].astype(jnp.bfloat16)
+            pair1_out[r, 1] = part1[i, 3].astype(jnp.bfloat16)
+            pairs[r] = send(pair1_out.at[r], pair1_in.at[r], sibling)
+    for r in order:
+        pairs[r].wait_recv()
+        summed = part1[place[r], 2] + pair1_in[r, 1].astype(jnp.float32)
+        cross_out[1, r] = summed.astype(jnp.bfloat16)
+        crosses[r] = send(cross_out.at[1, r], cross_in.at[1, r], across)
     returns = {}
     for r in order:
-        update = reduced(1, second_part, crosses, r)
+        crosses[r].wait_recv()
+        update = (
+            part1[place[r], 0]
+            + pair1_in[r, 0].astype(jnp.float32)
+            + cross_in[1, r].astype(jnp.float32)
+        )
         if r:
             back_out[r] = update.astype(jnp.bfloat16)
-            returns[r] = send(back_out.at[r], back_in.at[r], along(seq_size - r))
+            returns[r] = send(back_out.at[r], back_in.at[r], along(r))
         else:
             rows = current[r].astype(jnp.float32) + gate1 * update
             out_ref[0, chunk_rows(r), :] = rows.astype(jnp.bfloat16)
@@ -396,16 +425,17 @@
     head_dim = packed // 3
     tile = pixels // seq_size
     tokens = 4 * pixels
-    copies = 5 + 2 * 2 * seq_size + 2 * (seq_size - 1) + 3 * seq_size
+    copies = 6 + 4 * seq_size + 2 * (seq_size - 1) + 3 * seq_size
     anywhere = pl.BlockSpec(memory_space=pl.ANY)
     half, full = jnp.bfloat16, jnp.float32
     vmem = pltpu.VMEM
     return pl.pallas_call(
         functools.partial(fused_kernel, seq_size),
-        out_shape=jax.ShapeDtypeStruct(latents.shape, half),
-        in_specs=[pl.BlockSpec(memory_space=pltpu.SMEM)] + [anywhere] * 6,
+        out_shape=vmem(latents.shape, half),
+        in_specs=[anywhere] * 7,
         out_specs=pl.BlockSpec(memory_space=pltpu.VMEM),
         scratch_shapes=[
+            pltpu.SMEM(timestep.shape, jnp.int32),
             vmem(latents.shape, half),
             vmem((3, time_table.shape[0], width), full),
             vmem((3, blocks, width), full),
@@ -417,8 +447,10 @@
             vmem((heads * head_dim, tokens), full),
             vmem((4, seq_size, tile, width), full),
             vmem((seq_size, 4, tile, width), full),
-            vmem((blocks, seq_size, 2, tile, width), half),
-            vmem((blocks, seq_size, 2, tile, width), half),
+            vmem((2, seq_size, tile, width), half),
+            vmem((2, seq_size, tile, width), half),
+            vmem((seq_size, 2, tile, width), half),
+            vmem((seq_size, 2, tile, width), half),
             vmem((blocks, seq_size, tile, width), half),
             vmem((blocks, seq_size, tile, width), half),
             vmem((seq_size, tile, width), half),
@@ -426,12 +458,12 @@
             vmem((seq_size, 4, tile, width), half),
             vmem((seq_size, tile, width), half),
             vmem((seq_size, tile, width), half),
-            pltpu.SemaphoreType.DMA((8,)),
+            pltpu.SemaphoreType.DMA((9,)),
             pltpu.SemaphoreType.DMA((copies,)),
             pltpu.SemaphoreType.DMA((copies,)),
         ],
         compiler_params=pltpu.CompilerParams(
-            collective_id=0, has_side_effects=True, vmem_limit_bytes=67_043_328
+            collective_id=0, has_side_effects=True, vmem_limit_bytes=67_043_328 - 160 * 1024
         ),
     )(
         timestep,
@@ -452,7 +484,8 @@
         sizes["head"] == 2
         and sizes["sub"] == 2
         and frames == 1
-        and sizes["seq"] % 2 == 0
+        and sizes["seq"] > 1
+        and sizes["seq"] & (sizes["seq"] - 1) == 0
         and pixels % (16 * sizes["seq"]) == 0
         and pixels % 64 == 0
         and head_dim % 8 == 0

time: 41.5 us -> 39.2 us (0.945)
  Pallas kernels: 39.1 us -> 37.7 us
  local copies, waits for them, and re-layouts: 1.58 us -> 0.66 us
    pallas_call x1, Pallas kernels: 39.1 us -> 37.7 us  [fused_body(): pl.pallas_call(functools.partial(fused_kernel, seq_size), out_shape=vmem(...]
    unnamed x1, local copies, waits for them, and re-layouts: 1.58 us -> 0.66 us
where the time goes in v3:
time: 39.2 us; the launch traced here: 39 us
  Pallas kernels  37.7 us (96%)
  local copies, waits for them, and re-layouts  0.66 us (2%)
  between operations  0.66 us (2%)
    pallas_call x1, Pallas kernels, fused_body(): pl.pallas_call(functools.partial(fused_kernel, seq_size), out_shape=vmem(...  37.7 us

profile of v3, /device:TPU:0, one launch (start us, length us, event | category | flops | bytes accessed | tf_op | source)
XLA Modules:
  0.0 39.0 jit_solution(560669110253431349)
XLA Ops:
  0.7 37.7 %shard_map.73 = bf16[1,64,1152]{2,1,0:T(8,128)(2,1)S(1)} custom-call(s32[1]{0:T(128)S(6)} %copy.10.step_hbm, bf16[1,64,1152]{2,1,0:T(8,128)(2,1)} %lat_hbm.1, f32[3,30,1152]{2,1,0:T(8,128)} %bitcast.4, f32[3,2,1152]{2,1,0:T(2,128)} %bitcast.5, bf16[2,4,216,1152]{3,2,1,0:T(8,128)(2,1)} %bitcast.3, f32[2,2,72]{2,1,0:T(2,128)} %gain_hbm.1, ...), custom_call_target="tpu_custom_call" | custom-call | tf_op jit(solution)/shard_map/pallas_call | solution.py:432
  38.3 0.7 %copy.9 = bf16[1,64,1152]{2,1,0:T(8,128)(2,1)} copy(bf16[1,64,1152]{2,1,0:T(8,128)(2,1)S(1)} %shard_map.73) | data formatting | bytes 294912

commit v4 on v3

--- a/solution.py
+++ b/solution.py
@@ -353,7 +353,7 @@
     for i in range(1, seq_size):
         moves[by_place[i]].wait_recv()
         spread(i)
-    for i in range(seq_size - 1):
+    for i in range(seq_size):
         relay(i)
 
     def ready(places):
@@ -363,7 +363,6 @@
 
     ready(range(middle))
     project_block(1, g1[0:middle].reshape(2 * pixels, width), 0)
-    relay(seq_size - 1)
     ready(range(middle, seq_size))
     project_block(1, g1[middle:seq_size].reshape(2 * pixels, width), 1)
 

time: 39.2 us -> 38.1 us (0.972)
  Pallas kernels: 37.7 us -> 36.7 us
    pallas_call x1, Pallas kernels: 37.7 us -> 36.7 us  [fused_body(): pl.pallas_call(functools.partial(fused_kernel, seq_size), out_shape=vmem(...]
where the time goes in v4:
time: 38.1 us; the launch traced here: 38 us
  Pallas kernels  36.7 us (96%)
  local copies, waits for them, and re-layouts  0.66 us (2%)
  between operations  0.66 us (2%)
    pallas_call x1, Pallas kernels, fused_body(): pl.pallas_call(functools.partial(fused_kernel, seq_size), out_shape=vmem(...  36.7 us

profile of v4, /device:TPU:0, one launch (start us, length us, event | category | flops | bytes accessed | tf_op | source)
XLA Modules:
  0.0 38.0 jit_solution(6369130106926914947)
XLA Ops:
  0.7 36.7 %shard_map.73 = bf16[1,64,1152]{2,1,0:T(8,128)(2,1)S(1)} custom-call(s32[1]{0:T(128)S(6)} %copy.10.step_hbm, bf16[1,64,1152]{2,1,0:T(8,128)(2,1)} %lat_hbm.1, f32[3,30,1152]{2,1,0:T(8,128)} %bitcast.4, f32[3,2,1152]{2,1,0:T(2,128)} %bitcast.5, bf16[2,4,216,1152]{3,2,1,0:T(8,128)(2,1)} %bitcast.3, f32[2,2,72]{2,1,0:T(2,128)} %gain_hbm.1, ...), custom_call_target="tpu_custom_call" | custom-call | tf_op jit(solution)/shard_map/pallas_call | solution.py:431
  37.3 0.7 %copy.9 = bf16[1,64,1152]{2,1,0:T(8,128)(2,1)} copy(bf16[1,64,1152]{2,1,0:T(8,128)(2,1)S(1)} %shard_map.73) | data formatting | bytes 294912
